TPU v7x, 256 devices: a whole 4x4x8 slice. The times are simulated.
256 devices in a mesh: member: 16 (over y_lo, x, core), dp: 16 (over z, y_hi).
Axes of the slice: x: 4, y: 4 (y_hi: 2, y_lo: 2; y = y_hi * 2 + y_lo), z: 8, core: 2. Of those that a mesh axis runs over, the one named last changes fastest.
Arguments:
- trunk: bfloat16 [6304, 1024], P('dp'), may hold values from -6 to 6
- normgain: float32 [1024], replicated, may hold values from 0.25 to 1.75
- expand: bfloat16 [1024, 2048], P('member'), may hold values from -0.1875 to 0.1875
- shrink: bfloat16 [2048, 1024], P('member'), may hold values from -0.125 to 0.125
- inscale: float32 [16, 1024], P('member'), may hold values from 0.25 to 1.75
- hidscale: float32 [16, 2048], P('member'), may hold values from 0.25 to 1.75
- actscale: float32 [16, 2048], P('member'), may hold values from 0.25 to 1.75
- outscale: float32 [16, 1024], P('member'), may hold values from 0.25 to 1.75
- cotangent: bfloat16 [16, 6304, 1024], P('member', 'dp'), may hold values from -6 to 6
Outputs:
- trunk_grad: bfloat16 [6304, 1024], P('dp', 'member')
- expand_grad: float32 [1024, 2048], P('member')
- shrink_grad: float32 [2048, 1024], P('member')
- inscale_grad: float32 [16, 1024], P('member')
- hidscale_grad: float32 [16, 2048], P('member')
- actscale_grad: float32 [16, 2048], P('member')
- outscale_grad: float32 [16, 1024], P('member')
- normgain_grad: float32 [1024], replicated
All inputs are finite; a program needn't handle non-finite values.
Results may differ from a plain program's by a relative error of at most 0.024.
Values may be sent and summed in bfloat16 or wider, within the bound.
A program may use at most 64 MiB of HBM per device.

v0:
```python
import jax
import jax.numpy as jnp
from jax import lax
from jax.sharding import Mesh
from jax.sharding import PartitionSpec as P

MEMBER = ("member_0", "member_1", "member_2")
eps = 1e-06
coeff = 0.7978845608028654


def sent_to_all(x, axis):
    copies = jnp.broadcast_to(x, (lax.axis_size(axis), *x.shape))
    return lax.all_to_all(copies, axis, split_axis=0, concat_axis=0, tiled=True)


def joined_along(tiles, dim):
    tiles = jnp.moveaxis(tiles, 0, dim)
    dims = tiles.shape
    return tiles.reshape(*dims[:dim], dims[dim] * dims[dim + 1], *dims[dim + 2 :])


def gathered_by_axis(x, axes, dim):
    far, near = axes
    tiles = sent_to_all(sent_to_all(x, far), near)
    return joined_along(tiles.swapaxes(0, 1).reshape(-1, *x.shape), dim)


def split_up(x, dim, peers):
    before, after = (x.shape[:dim], x.shape[dim + 1 :])
    return jnp.moveaxis(x.reshape(*before, peers, -1, *after), dim, 0)


def sent_and_summed(x, axis, dim):
    tiles = split_up(x, dim, lax.axis_size(axis))
    arrived = lax.all_to_all(tiles, axis, split_axis=0, concat_axis=0, tiled=True)
    return arrived.astype(jnp.float32).sum(axis=0)


def summed_rows(x, axes, dim):
    far, near = axes
    tiles = split_up(x, dim, lax.axis_size(far))
    nearer = sent_and_summed(tiles, near, dim + 1)
    arrived = lax.all_to_all(
        nearer.astype(jnp.bfloat16), far, split_axis=0, concat_axis=0, tiled=True
    )
    return arrived.astype(jnp.float32).sum(axis=0)


def filled_up(lines, peers):
    spare = -len(lines) % peers
    return jnp.pad(lines, [(0, spare)] + [(0, 0)] * (lines.ndim - 1))


def collect(x, axis, dim):
    return joined_along(sent_to_all(x, axis), dim)


def sum_by_parts(x, axes):
    lines = x.reshape(-1, x.shape[-1])
    own = sent_and_summed(filled_up(lines, lax.axis_size(axes)), axes, 0)
    whole = collect(own.astype(jnp.bfloat16), axes, 0)
    return whole[: len(lines)].reshape(x.shape).astype(jnp.float32)


def over_copies(x, axis):
    return sent_to_all(x, axis).sum(axis=0)


def in_one(arrays, axis):
    ends = [0]
    for a in arrays:
        ends.append(ends[-1] + a.size)
    total = over_copies(jnp.concatenate([a.ravel() for a in arrays]), axis)
    return tuple((total[b:e].reshape(a.shape) for a, b, e in zip(arrays, ends, ends[1:])))


def gelu_pair(hidden):
    inner = coeff * (hidden + 0.044715 * hidden * hidden * hidden)
    tangent = jnp.tanh(inner)
    active = 0.5 * hidden * (1.0 + tangent)
    slope = 0.5 * (1.0 + tangent) + 0.5 * hidden * (1.0 - tangent * tangent) * coeff * (
        1.0 + 3.0 * 0.044715 * hidden * hidden
    )
    return (active, slope)


def rounded_term(left, right):
    term = lax.dot_general(
        left, right, (((0,), (0,)), ((), ())), preferred_element_type=jnp.float32
    )
    return lax.optimization_barrier(term.astype(jnp.bfloat16)).astype(jnp.float32)


def body(trunk, normgain, expand, shrink, inscale, hidscale, actscale, outscale, cotangent):
    scale_in = inscale[0]
    scale_hid = hidscale[0]
    scale_act = actscale[0]
    scale_out = outscale[0]
    tokens = trunk.astype(jnp.float32)
    centered = tokens - jnp.mean(tokens, axis=1, keepdims=True)
    variance = jnp.mean(centered * centered, axis=1, keepdims=True)
    inv_std = lax.rsqrt(variance + eps)
    normed = centered * inv_std
    gained = normed * normgain
    scaled_in = (gained * scale_in).astype(jnp.bfloat16)
    expand_full = lax.all_gather(expand, MEMBER, axis=0, tiled=True)
    project = jnp.dot(scaled_in, expand_full, preferred_element_type=jnp.float32)
    hidden = project * scale_hid
    active, slope = gelu_pair(hidden)
    scaled_act = (active * scale_act).astype(jnp.bfloat16)
    upstream = cotangent[0].astype(jnp.float32)
    scaled_cot = (upstream * scale_out).astype(jnp.bfloat16)
    piece = gathered_by_axis(shrink, (("member_0", "member_1"), "member_2"), 0)
    second = jnp.dot(scaled_act, piece, preferred_element_type=jnp.float32)
    back = lax.dot_general(
        scaled_cot, piece, (((1,), (1,)), ((), ())), preferred_element_type=jnp.float32
    )
    back_act = back
    second, back_act = (second, back_act)
    grad_out = jnp.sum(upstream * second, axis=0)
    grad_act = jnp.sum(back_act * active, axis=0)
    back_hidden = back_act * scale_act * slope
    grad_hid = jnp.sum(back_hidden * project, axis=0)
    back_proj = (back_hidden * scale_hid).astype(jnp.bfloat16)
    expand_part = summed_rows(
        rounded_term(scaled_in, back_proj).astype(jnp.bfloat16),
        (("member_0", "member_1"), "member_2"),
        0,
    )
    shrink_part = summed_rows(
        rounded_term(scaled_act, scaled_cot).astype(jnp.bfloat16),
        (("member_0", "member_1"), "member_2"),
        0,
    )
    expand_grad, shrink_grad = (
        sum_by_parts(expand_part.astype(jnp.bfloat16), "dp"),
        sum_by_parts(shrink_part.astype(jnp.bfloat16), "dp"),
    )
    back_norm = lax.dot_general(
        back_proj, expand_full, (((1,), (1,)), ((), ())), preferred_element_type=jnp.float32
    )
    grad_in = jnp.sum(back_norm * gained, axis=0)
    back_scaled = back_norm * scale_in
    gain_term = jnp.sum(back_scaled * normed, axis=0)
    back_unit = back_scaled * normgain
    back_trunk = inv_std * (
        back_unit
        - jnp.mean(back_unit, axis=1, keepdims=True)
        - normed * jnp.mean(back_unit * normed, axis=1, keepdims=True)
    )
    member_term = upstream + back_trunk
    trunk_grad = sent_and_summed(member_term.astype(jnp.bfloat16), MEMBER, 1).astype(jnp.bfloat16)
    grad_in, grad_hid, grad_act, grad_out, gain_shard = in_one(
        (grad_in, grad_hid, grad_act, grad_out, gain_term), "dp"
    )
    gain_grad = over_copies(gain_shard, MEMBER)
    return (
        trunk_grad,
        expand_grad,
        shrink_grad,
        grad_in[None],
        grad_hid[None],
        grad_act[None],
        grad_out[None],
        gain_grad,
    )


def solution(mesh):
    finer = Mesh(
        mesh.devices.reshape(2, 4, 2, mesh.shape["dp"]), ("member_0", "member_1", "member_2", "dp")
    )
    in_specs = (
        P("dp", None),
        P(),
        P(MEMBER, None),
        P(MEMBER, None),
        P(MEMBER, None),
        P(MEMBER, None),
        P(MEMBER, None),
        P(MEMBER, None),
        P(MEMBER, "dp", None),
    )
    out_specs = (
        P("dp", MEMBER),
        P(MEMBER, None),
        P(MEMBER, None),
        P(MEMBER, None),
        P(MEMBER, None),
        P(MEMBER, None),
        P(MEMBER, None),
        P(),
    )
    return jax.shard_map(body, mesh=finer, in_specs=in_specs, out_specs=out_specs, check_vma=False)
```

profile of v0, /device:TPU:8, one launch (start us, length us, event | category | flops | bytes accessed | tf_op | source)
XLA Modules:
  0.0 317.4 jit_solution(12734090389983294515)
XLA Ops:
  7.9 2.6 broadcast_in_dim.36
  10.5 5.8 %all-to-all-start = ((bf16[8,128,1024]{2,1,0:T(8,128)(2,1)}), bf16[8,128,1024]{2,1,0:T(8,128)(2,1)S(1)}, u32[]{:S(2)}, u32[]{:S(2)}) async-start(bf16[8,128,1024]{2,1,0:T(8,128)(2,1)} %broadcast_in_dim.36), calls=%async_computation | async-start | bytes 4194304 | tf_op jit(solution)/shard_map/all_to_all | solution.py:14
  16.9 27.5 %all-to-all-done = bf16[8,128,1024]{2,1,0:T(8,128)(2,1)S(1)} async-done(((bf16[8,128,1024]{2,1,0:T(8,128)(2,1)}), bf16[8,128,1024]{2,1,0:T(8,128)(2,1)S(1)}, u32[]{:S(2)}, u32[]{:S(2)}) %all-to-all-start) | async-done | bytes 2097184 | tf_op jit(solution)/shard_map/all_to_all | solution.py:14
  44.8 7.5 %all_to_all.67 = bf16[2,8,128,1024]{3,2,1,0:T(8,128)(2,1)S(1)} all-to-all(bf16[2,8,128,1024]{3,2,1,0:T(8,128)(2,1)S(1)} %broadcast_in_dim.37), channel_id=1, replica_groups=mesh['member_0'=2,'member_1'=4,'member_2'=2,'dp'=16] {'member_2'}, dimensions={0} | all-to-all | bytes 8388608 | tf_op jit(solution)/shard_map/all_to_all | solution.py:14
  54.8 10.6 %all-gather.2.cloned.1.call-done = bf16[1024,2048]{1,0:T(8,128)(2,1)} async-done(((bf16[64,2048]{1,0:T(8,128)(2,1)}), bf16[1024,2048]{1,0:T(8,128)(2,1)}) %all-gather.2.cloned.1.call-update) | async-done | bytes 4194320 | tf_op jit(solution)/shard_map/all_gather | solution.py:107
  65.4 4.3 %fusion.37 = f32[394,2048]{1,0:T(8,128)S(1)} fusion(bf16[1024,2048]{1,0:T(8,128)(2,1)} %all-gather.2.cloned.1.call-done, bf16[394,1024]{1,0:T(8,128)(2,1)S(1)} %copy-done.1, f32[1024]{0:T(1024)S(1)} %bitcast.60, f32[1024]{0:T(1024)S(1)} %copy-done.5, f32[394]{0:T(512)S(1)} %add_rsqrt_fusion, f32[394]{0:T(512)S(1)} %broadcast_multiply_fusion.2), kind=kOutput, calls=%fused_computation.60 | convolution fusion | flops 1654976512 | bytes 8240208 | tf_op jit(solution)/shard_map/dot_general | solution.py:108
  72.2 4.2 %multiply_reduce_fusion = (f32[2048]{0:T(1024)S(1)}, f32[2048]{0:T(1024)S(1)}, f32[394,2048]{1,0:T(8,128)S(1)}) fusion(f32[394,2048]{1,0:T(8,128)S(1)} %fusion.37, f32[2048]{0:T(1024)S(1)} %bitcast.65, f32[2048]{0:T(1024)S(1)} %bitcast.70, bf16[2048,1024]{1,0:T(8,128)(2,1)S(1)} %bitcast.55, bf16[1,394,1024]{2,1,0:T(8,128)(2,1)S(1)} %copy-done.3, ...), kind=kOutput, calls=%fused_computation.12 | convolution fusion | flops 1673934848 | bytes 11493376 | tf_op jit(solution)/shard_map/dot_general | solution.py:116
  76.4 5.0 %convolution_convert_fusion = bf16[2048,1024]{1,0:T(8,128)(2,1)} fusion(bf16[1,394,1024]{2,1,0:T(8,128)(2,1)S(1)} %copy-done.3, f32[1024]{0:T(1024)S(1)} %bitcast.75, f32[2048]{0:T(1024)S(1)} %bitcast.71, f32[394,2048]{1,0:T(8,128)S(1)} %fusion.37, f32[2048]{0:T(1024)S(1)} %bitcast.66), kind=kOutput, calls=%fused_computation.4 | convolution fusion | flops 1664739328 | bytes 8249344 | tf_op jit(solution)/shard_map/dot_general | solution.py:89
  81.4 4.5 %convolution_convert_fusion.1 = bf16[1024,2048]{1,0:T(8,128)(2,1)S(1)} fusion(f32[2048]{0:T(1024)S(1)} %bitcast.67, bf16[394,1024]{1,0:T(8,128)(2,1)S(1)} %copy-done.1, f32[1024]{0:T(1024)S(1)} %bitcast.61, f32[1024]{0:T(1024)S(1)} %copy-done.5, f32[394]{0:T(512)S(1)} %add_rsqrt_fusion, f32[394]{0:T(512)S(1)} %broadcast_multiply_fusion.2, ...), kind=kOutput, calls=%fused_computation.5 | convolution fusion | flops 1674825728 | bytes 11484240 | tf_op jit(solution)/shard_map/dot_general | solution.py:89
  85.9 5.2 %fusion.22 = (f32[1024]{0:T(1024)S(1)}, f32[394]{0:T(512)S(1)}, f32[1024]{0:T(1024)S(1)}, f32[394]{0:T(512)S(1)}, f32[394,1024]{1,0:T(8,128)}) fusion(bf16[394,1024]{1,0:T(8,128)(2,1)S(1)} %copy-done.1, f32[1024]{0:T(1024)S(1)} %bitcast.62, f32[394]{0:T(512)S(1)} %add_rsqrt_fusion, f32[394]{0:T(512)S(1)} %broadcast_multiply_fusion.2, ...), kind=kOutput, calls=%fused_computation.37 | convolution fusion | flops 1675549952 | bytes 13109408 | tf_op jit(solution)/shard_map/dot_general | solution.py:140
  93.4 5.6 %all-to-all-start.3 = ((bf16[2,8,64,2048]{3,2,1,0:T(8,128)(2,1)}), bf16[2,8,64,2048]{3,2,1,0:T(8,128)(2,1)}, u32[]{:S(2)}, u32[]{:S(2)}) async-start(bf16[2,8,64,2048]{3,2,1,0:T(8,128)(2,1)} %bitcast.50), calls=%async_computation.3 | async-start | bytes 8388608 | tf_op jit(solution)/shard_map/all_to_all | solution.py:36
  99.0 4.8 %copy.44 = bf16[8,2,128,1024]{3,2,0,1:T(8,128)(2,1)} copy(bf16[8,2,128,1024]{3,2,1,0:T(8,128)(2,1)} %bitcast.52) | data formatting | bytes 8388608 | tf_op jit(solution)/shard_map/reshape;reshape | solution.py:31
  103.8 11.9 %all_to_all.68 = bf16[2,8,128,1024]{3,2,1,0:T(8,128)(2,1)} all-to-all(bf16[2,8,128,1024]{3,2,1,0:T(8,128)(2,1)} %bitcast.51), channel_id=1, replica_groups=mesh['member_0'=2,'member_1'=4,'member_2'=2,'dp'=16] {'member_2'}, dimensions={0} | all-to-all | bytes 8388608 | tf_op jit(solution)/shard_map/all_to_all | solution.py:36
  116.7 10.2 %all-to-all-start.11 = ((f32[16,1,7168]{2,1,0:T(1,128)}), f32[16,1,7168]{2,1,0:T(1,128)S(1)}, u32[]{:S(2)}, u32[]{:S(2)}) async-start(f32[16,1,7168]{2,1,0:T(1,128)} %broadcast_in_dim.40), calls=%async_computation.11 | async-start | bytes 917504 | tf_op jit(solution)/shard_map/all_to_all | solution.py:14
  130.4 14.5 %all-to-all-done.11 = f32[16,1,7168]{2,1,0:T(1,128)S(1)} async-done(((f32[16,1,7168]{2,1,0:T(1,128)}), f32[16,1,7168]{2,1,0:T(1,128)S(1)}, u32[]{:S(2)}, u32[]{:S(2)}) %all-to-all-start.11) | async-done | bytes 458784 | tf_op jit(solution)/shard_map/all_to_all | solution.py:14
  145.0 5.4 %all-to-all-start.2 = ((bf16[16,394,64]{1,2,0:T(8,128)(2,1)}), bf16[16,394,64]{1,2,0:T(8,128)(2,1)S(1)}, u32[]{:S(2)}, u32[]{:S(2)}) async-start(bf16[16,394,64]{1,2,0:T(8,128)(2,1)} %bitcast.9), calls=%async_computation.2 | async-start | bytes 2097152 | tf_op jit(solution)/shard_map/all_to_all | solution.py:36
  151.3 14.2 %all-to-all-done.2 = bf16[16,394,64]{1,2,0:T(8,128)(2,1)S(1)} async-done(((bf16[16,394,64]{1,2,0:T(8,128)(2,1)}), bf16[16,394,64]{1,2,0:T(8,128)(2,1)S(1)}, u32[]{:S(2)}, u32[]{:S(2)}) %all-to-all-start.2) | async-done | bytes 806944 | tf_op jit(solution)/shard_map/all_to_all | solution.py:36
  166.2 4.9 %all-to-all-start.12 = ((f32[16,1,1024]{2,1,0:T(1,128)}), f32[16,1,1024]{2,1,0:T(1,128)S(1)}, u32[]{:S(2)}, u32[]{:S(2)}) async-start(f32[16,1,1024]{2,1,0:T(1,128)} %broadcast_in_dim.45), calls=%async_computation.12 | async-start | bytes 131072 | tf_op jit(solution)/shard_map/all_to_all | solution.py:14
  171.0 5.2 %reduce_sum.188 = bf16[8,64,2048]{2,1,0:T(8,128)(2,1)} reduce(bf16[2,8,64,2048]{3,2,1,0:T(8,128)(2,1)} %all-to-all-done.3, bf16[]{:T(256)} %constant.28.clone.1), dimensions={0}, to_apply=%region_5.0 | reduce | flops 1048576 | bytes 6291458 | tf_op jit(solution)/shard_map/reduce_sum | solution.py:37
  176.2 5.7 %all-to-all-start.4 = ((bf16[8,64,2048]{2,1,0:T(8,128)(2,1)}), bf16[8,64,2048]{2,1,0:T(8,128)(2,1)S(1)}, u32[]{:S(2)}, u32[]{:S(2)}) async-start(bf16[8,64,2048]{2,1,0:T(8,128)(2,1)} %reduce_sum.188), calls=%async_computation.4 | async-start | bytes 4194304 | tf_op jit(solution)/shard_map/all_to_all | solution.py:44
  181.9 5.2 %reduce_sum.191 = bf16[8,128,1024]{2,1,0:T(8,128)(2,1)} reduce(bf16[2,8,128,1024]{3,2,1,0:T(8,128)(2,1)} %all_to_all.68, bf16[]{:T(256)} %constant.28.clone.1), dimensions={0}, to_apply=%region_8.0 | reduce | flops 1048576 | bytes 6291458 | tf_op jit(solution)/shard_map/reduce_sum | solution.py:37
  187.2 20.5 %all-to-all-done.4 = bf16[8,64,2048]{2,1,0:T(8,128)(2,1)S(1)} async-done(((bf16[8,64,2048]{2,1,0:T(8,128)(2,1)}), bf16[8,64,2048]{2,1,0:T(8,128)(2,1)S(1)}, u32[]{:S(2)}, u32[]{:S(2)}) %all-to-all-start.4) | async-done | bytes 2097184 | tf_op jit(solution)/shard_map/all_to_all | solution.py:44
  209.0 8.7 %all-to-all-start.8 = ((bf16[8,128,1024]{2,1,0:T(8,128)(2,1)}), bf16[8,128,1024]{2,1,0:T(8,128)(2,1)S(1)}, u32[]{:S(2)}, u32[]{:S(2)}) async-start(bf16[8,128,1024]{2,1,0:T(8,128)(2,1)} %reduce_sum.191), calls=%async_computation.8 | async-start | bytes 4194304 | tf_op jit(solution)/shard_map/all_to_all | solution.py:44
  220.4 21.8 %all-to-all-done.8 = bf16[8,128,1024]{2,1,0:T(8,128)(2,1)S(1)} async-done(((bf16[8,128,1024]{2,1,0:T(8,128)(2,1)}), bf16[8,128,1024]{2,1,0:T(8,128)(2,1)S(1)}, u32[]{:S(2)}, u32[]{:S(2)}) %all-to-all-start.8) | async-done | bytes 2097184 | tf_op jit(solution)/shard_map/all_to_all | solution.py:44
  242.2 3.5 %all-to-all-start.5 = ((bf16[16,4,2048]{2,1,0:T(4,128)(2,1)}), bf16[16,4,2048]{2,1,0:T(4,128)(2,1)S(1)}, u32[]{:S(2)}, u32[]{:S(2)}) async-start(bf16[16,4,2048]{2,1,0:T(4,128)(2,1)} %reshape.70), calls=%async_computation.5 | async-start | bytes 524288 | tf_op jit(solution)/shard_map/all_to_all | solution.py:36
  246.9 13.0 %all-to-all-done.5 = bf16[16,4,2048]{2,1,0:T(4,128)(2,1)S(1)} async-done(((bf16[16,4,2048]{2,1,0:T(4,128)(2,1)}), bf16[16,4,2048]{2,1,0:T(4,128)(2,1)S(1)}, u32[]{:S(2)}, u32[]{:S(2)}) %all-to-all-start.5) | async-done | bytes 262176 | tf_op jit(solution)/shard_map/all_to_all | solution.py:36
  259.9 3.5 %all-to-all-start.9 = ((bf16[16,8,1024]{2,1,0:T(8,128)(2,1)}), bf16[16,8,1024]{2,1,0:T(8,128)(2,1)S(1)}, u32[]{:S(2)}, u32[]{:S(2)}) async-start(bf16[16,8,1024]{2,1,0:T(8,128)(2,1)} %bitcast.14), calls=%async_computation.9 | async-start | bytes 524288 | tf_op jit(solution)/shard_map/all_to_all | solution.py:36
  263.5 12.4 %all-to-all-done.9 = bf16[16,8,1024]{2,1,0:T(8,128)(2,1)S(1)} async-done(((bf16[16,8,1024]{2,1,0:T(8,128)(2,1)}), bf16[16,8,1024]{2,1,0:T(8,128)(2,1)S(1)}, u32[]{:S(2)}, u32[]{:S(2)}) %all-to-all-start.9) | async-done | bytes 262176 | tf_op jit(solution)/shard_map/all_to_all | solution.py:36
  276.8 3.5 %all-to-all-start.6 = ((bf16[16,4,2048]{2,1,0:T(4,128)(2,1)}), bf16[16,4,2048]{2,1,0:T(4,128)(2,1)S(1)}, u32[]{:S(2)}, u32[]{:S(2)}) async-start(bf16[16,4,2048]{2,1,0:T(4,128)(2,1)} %broadcast_in_dim.38), calls=%async_computation.6 | async-start | bytes 524288 | tf_op jit(solution)/shard_map/all_to_all | solution.py:14
  280.4 12.5 %all-to-all-done.6 = bf16[16,4,2048]{2,1,0:T(4,128)(2,1)S(1)} async-done(((bf16[16,4,2048]{2,1,0:T(4,128)(2,1)}), bf16[16,4,2048]{2,1,0:T(4,128)(2,1)S(1)}, u32[]{:S(2)}, u32[]{:S(2)}) %all-to-all-start.6) | async-done | bytes 262176 | tf_op jit(solution)/shard_map/all_to_all | solution.py:14
  293.6 3.5 %all-to-all-start.10 = ((bf16[16,8,1024]{2,1,0:T(8,128)(2,1)}), bf16[16,8,1024]{2,1,0:T(8,128)(2,1)S(1)}, u32[]{:S(2)}, u32[]{:S(2)}) async-start(bf16[16,8,1024]{2,1,0:T(8,128)(2,1)} %broadcast_in_dim.39), calls=%async_computation.10 | async-start | bytes 524288 | tf_op jit(solution)/shard_map/all_to_all | solution.py:14
  300.0 9.7 %all-to-all-done.10 = bf16[16,8,1024]{2,1,0:T(8,128)(2,1)S(1)} async-done(((bf16[16,8,1024]{2,1,0:T(8,128)(2,1)}), bf16[16,8,1024]{2,1,0:T(8,128)(2,1)S(1)}, u32[]{:S(2)}, u32[]{:S(2)}) %all-to-all-start.10) | async-done | bytes 262176 | tf_op jit(solution)/shard_map/all_to_all | solution.py:14
  (56 shorter events, 25.6 us)
Async XLA Ops:
  7.2 58.2 %all-gather.2.cloned.1.call-start = ((), (), s32[]{:S(2)}) async-start(), calls=%async_computation.13 | async-start | bytes 4456448 | tf_op jit(solution)/shard_map/all_gather | solution.py:107
  7.9 8.4 %copy-start.1 = (bf16[394,1024]{1,0:T(8,128)(2,1)S(1)}, bf16[394,1024]{1,0:T(8,128)(2,1)}, u32[]{:S(2)}) copy-start(bf16[394,1024]{1,0:T(8,128)(2,1)} %param.9) | copy-start | bytes 2420740
  10.5 33.8 %all-to-all-start = ((bf16[8,128,1024]{2,1,0:T(8,128)(2,1)}), bf16[8,128,1024]{2,1,0:T(8,128)(2,1)S(1)}, u32[]{:S(2)}, u32[]{:S(2)}) async-start(bf16[8,128,1024]{2,1,0:T(8,128)(2,1)} %broadcast_in_dim.36), calls=%async_computation | async-start | bytes 4194304 | tf_op jit(solution)/shard_map/all_to_all | solution.py:14
  52.4 13.0 %copy-start.4 = (f32[1,1024]{1,0:T(1,128)S(1)}, f32[1,1024]{1,0:T(1,128)}, u32[]{:S(2)}) copy-start(f32[1,1024]{1,0:T(1,128)} %param.13) | copy-start | bytes 12292
  52.4 13.0 %copy-start.5 = (f32[1024]{0:T(1024)S(1)}, f32[1024]{0:T(1024)}, u32[]{:S(2)}) copy-start(f32[1024]{0:T(1024)} %param.10) | copy-start | bytes 12292
  65.4 4.4 %copy-start.2 = (bf16[2,8,128,1024]{3,2,0,1:T(8,128)(2,1)S(1)}, bf16[2,8,128,1024]{3,2,0,1:T(8,128)(2,1)}, u32[]{:S(2)}) copy-start(bf16[2,8,128,1024]{3,2,0,1:T(8,128)(2,1)} %copy.27) | copy-start | bytes 12582916
  65.4 4.4 %copy-start.3 = (bf16[1,394,1024]{2,1,0:T(8,128)(2,1)S(1)}, bf16[1,394,1024]{2,1,0:T(8,128)(2,1)}, u32[]{:S(2)}) copy-start(bf16[1,394,1024]{2,1,0:T(8,128)(2,1)} %param.17) | copy-start | bytes 2420740
  65.4 4.4 %copy-start.7 = (f32[1,2048]{1,0:T(1,128)S(1)}, f32[1,2048]{1,0:T(1,128)}, u32[]{:S(2)}) copy-start(f32[1,2048]{1,0:T(1,128)} %param.14) | copy-start | bytes 24580
  65.4 4.4 %copy-start.8 = (f32[1,2048]{1,0:T(1,128)S(1)}, f32[1,2048]{1,0:T(1,128)}, u32[]{:S(2)}) copy-start(f32[1,2048]{1,0:T(1,128)} %param.15) | copy-start | bytes 24580
  69.7 2.4 copy-start.9
  81.4 4.6 %copy-start.6 = (bf16[1024,2048]{1,0:T(8,128)(2,1)S(1)}, bf16[1024,2048]{1,0:T(8,128)(2,1)}, u32[]{:S(2)}) copy-start(bf16[1024,2048]{1,0:T(8,128)(2,1)} %all-gather.2.cloned.1.call-done) | copy-start | bytes 12582916
  93.4 10.4 %all-to-all-start.3 = ((bf16[2,8,64,2048]{3,2,1,0:T(8,128)(2,1)}), bf16[2,8,64,2048]{3,2,1,0:T(8,128)(2,1)}, u32[]{:S(2)}, u32[]{:S(2)}) async-start(bf16[2,8,64,2048]{3,2,1,0:T(8,128)(2,1)} %bitcast.50), calls=%async_computation.3 | async-start | bytes 8388608 | tf_op jit(solution)/shard_map/all_to_all | solution.py:36
  116.7 28.3 %all-to-all-start.11 = ((f32[16,1,7168]{2,1,0:T(1,128)}), f32[16,1,7168]{2,1,0:T(1,128)S(1)}, u32[]{:S(2)}, u32[]{:S(2)}) async-start(f32[16,1,7168]{2,1,0:T(1,128)} %broadcast_in_dim.40), calls=%async_computation.11 | async-start | bytes 917504 | tf_op jit(solution)/shard_map/all_to_all | solution.py:14
  145.0 20.5 %all-to-all-start.2 = ((bf16[16,394,64]{1,2,0:T(8,128)(2,1)}), bf16[16,394,64]{1,2,0:T(8,128)(2,1)S(1)}, u32[]{:S(2)}, u32[]{:S(2)}) async-start(bf16[16,394,64]{1,2,0:T(8,128)(2,1)} %bitcast.9), calls=%async_computation.2 | async-start | bytes 2097152 | tf_op jit(solution)/shard_map/all_to_all | solution.py:36
  166.2 10.0 %all-to-all-start.12 = ((f32[16,1,1024]{2,1,0:T(1,128)}), f32[16,1,1024]{2,1,0:T(1,128)S(1)}, u32[]{:S(2)}, u32[]{:S(2)}) async-start(f32[16,1,1024]{2,1,0:T(1,128)} %broadcast_in_dim.45), calls=%async_computation.12 | async-start | bytes 131072 | tf_op jit(solution)/shard_map/all_to_all | solution.py:14
  176.2 31.5 %all-to-all-start.4 = ((bf16[8,64,2048]{2,1,0:T(8,128)(2,1)}), bf16[8,64,2048]{2,1,0:T(8,128)(2,1)S(1)}, u32[]{:S(2)}, u32[]{:S(2)}) async-start(bf16[8,64,2048]{2,1,0:T(8,128)(2,1)} %reduce_sum.188), calls=%async_computation.4 | async-start | bytes 4194304 | tf_op jit(solution)/shard_map/all_to_all | solution.py:44
  207.7 1.3 copy-start
  209.0 33.2 %all-to-all-start.8 = ((bf16[8,128,1024]{2,1,0:T(8,128)(2,1)}), bf16[8,128,1024]{2,1,0:T(8,128)(2,1)S(1)}, u32[]{:S(2)}, u32[]{:S(2)}) async-start(bf16[8,128,1024]{2,1,0:T(8,128)(2,1)} %reduce_sum.191), calls=%async_computation.8 | async-start | bytes 4194304 | tf_op jit(solution)/shard_map/all_to_all | solution.py:44
  242.2 17.6 %all-to-all-start.5 = ((bf16[16,4,2048]{2,1,0:T(4,128)(2,1)}), bf16[16,4,2048]{2,1,0:T(4,128)(2,1)S(1)}, u32[]{:S(2)}, u32[]{:S(2)}) async-start(bf16[16,4,2048]{2,1,0:T(4,128)(2,1)} %reshape.70), calls=%async_computation.5 | async-start | bytes 524288 | tf_op jit(solution)/shard_map/all_to_all | solution.py:36
  259.9 16.1 %all-to-all-start.9 = ((bf16[16,8,1024]{2,1,0:T(8,128)(2,1)}), bf16[16,8,1024]{2,1,0:T(8,128)(2,1)S(1)}, u32[]{:S(2)}, u32[]{:S(2)}) async-start(bf16[16,8,1024]{2,1,0:T(8,128)(2,1)} %bitcast.14), calls=%async_computation.9 | async-start | bytes 524288 | tf_op jit(solution)/shard_map/all_to_all | solution.py:36
  276.8 16.1 %all-to-all-start.6 = ((bf16[16,4,2048]{2,1,0:T(4,128)(2,1)}), bf16[16,4,2048]{2,1,0:T(4,128)(2,1)S(1)}, u32[]{:S(2)}, u32[]{:S(2)}) async-start(bf16[16,4,2048]{2,1,0:T(4,128)(2,1)} %broadcast_in_dim.38), calls=%async_computation.6 | async-start | bytes 524288 | tf_op jit(solution)/shard_map/all_to_all | solution.py:14
  293.6 16.1 %all-to-all-start.10 = ((bf16[16,8,1024]{2,1,0:T(8,128)(2,1)}), bf16[16,8,1024]{2,1,0:T(8,128)(2,1)S(1)}, u32[]{:S(2)}, u32[]{:S(2)}) async-start(bf16[16,8,1024]{2,1,0:T(8,128)(2,1)} %broadcast_in_dim.39), calls=%async_computation.10 | async-start | bytes 524288 | tf_op jit(solution)/shard_map/all_to_all | solution.py:14
Sparse Core Ops, SparseCore 0:
  9.8 55.4 all-gather.1
where the time goes:
time: 319 us; the launch traced here: 317 us
  waiting for transfers between devices  157 us (49%)
  starting transfers between devices  60.5 us (19%)
  matrix products  25.6 us (8%)
  local copies, waits for them, and re-layouts  21.3 us (7%)
  blocking collectives  19.4 us (6%)
  other arithmetic  18.9 us (6%)
  between operations  14.3 us (4%)
    all_to_all x5, waiting for transfers between devices, sent_to_all(): return lax.all_to_all(copies, axis, split_axis=0, concat_axis=0, tiled=True)  64.2 us
    all_to_all x2, waiting for transfers between devices, summed_rows(): lax.all_to_all(nearer.astype(jnp.bfloat16), far, split_axis=0, concat_axi...  42.3 us
    all_to_all x4, waiting for transfers between devices, sent_and_summed(): lax.all_to_all(tiles, axis, split_axis=0, concat_axis=0, tiled=True)  39.6 us
    all_to_all x5, starting transfers between devices, sent_to_all(): return lax.all_to_all(copies, axis, split_axis=0, concat_axis=0, tiled=True)  27.9 us
    all_to_all x4, starting transfers between devices, sent_and_summed(): lax.all_to_all(tiles, axis, split_axis=0, concat_axis=0, tiled=True)  18.1 us
    all_to_all x2, starting transfers between devices, summed_rows(): lax.all_to_all(nearer.astype(jnp.bfloat16), far, split_axis=0, concat_axi...  14.4 us
    all_to_all x1, blocking collectives, sent_and_summed(): lax.all_to_all(tiles, axis, split_axis=0, concat_axis=0, tiled=True)  11.9 us
    reduce_sum x5, other arithmetic, sent_and_summed(): return arrived.astype(jnp.float32).sum(axis=0)  11.4 us
  transfers between devices with their start and end apart: 12, of which 10 were waited for; matrix products, arithmetic and copies ran while one was open for 10% of the time, Pallas kernels for 0%

commit v1 on v0

--- a/solution.py
+++ b/solution.py
@@ -104,7 +104,9 @@
     normed = centered * inv_std
     gained = normed * normgain
     scaled_in = (gained * scale_in).astype(jnp.bfloat16)
-    expand_full = lax.all_gather(expand, MEMBER, axis=0, tiled=True)
+    top = jnp.stack([expand for _ in range(lax.psum(1, MEMBER))], axis=0)
+    u_next = lax.all_to_all(top, MEMBER, 0, 0)
+    expand_full = jnp.concatenate(u_next, 0)
     project = jnp.dot(scaled_in, expand_full, preferred_element_type=jnp.float32)
     hidden = project * scale_hid
     active, slope = gelu_pair(hidden)

time: 319 us -> 355 us (1.11)
  blocking collectives: 19.4 us -> 51.3 us
  between operations: 14.3 us -> 0.89 us
  waiting for transfers between devices: 157 us -> 169 us
    all_to_all x0 -> x1, waiting for transfers between devices: none -> 50.2 us  [body(): u_next = lax.all_to_all(top, MEMBER, 0, 0)]
    all_to_all x1 -> x2, blocking collectives: 7.52 us -> 39.4 us  [sent_to_all(): return lax.all_to_all(copies, axis, split_axis=0, concat_axis=0, tiled=True)]
    all_to_all x5 -> x4, waiting for transfers between devices: 64.2 us -> 36.7 us  [sent_to_all(): return lax.all_to_all(copies, axis, split_axis=0, concat_axis=0, tiled=True)]
    all_gather x1 -> x0, waiting for transfers between devices: 10.6 us -> none  [body(): expand_full = lax.all_gather(expand, MEMBER, axis=0, tiled=True)]
    all_to_all x0 -> x1, starting transfers between devices: none -> 5.9 us  [body(): u_next = lax.all_to_all(top, MEMBER, 0, 0)]
    all_to_all x5 -> x4, starting transfers between devices: 27.9 us -> 22.2 us  [sent_to_all(): return lax.all_to_all(copies, axis, split_axis=0, concat_axis=0, tiled=True)]
  transfers between devices with their start and end apart: 12 -> 11, of which waited for: 10 -> 9; matrix products, arithmetic and copies ran while one was open for 10% -> 9% of each run, Pallas kernels for 0% -> 0%
where the time goes in v1:
time: 355 us; the launch traced here: 353 us
  waiting for transfers between devices  169 us (48%)
  starting transfers between devices  60.4 us (17%)
  blocking collectives  51.3 us (14%)
  matrix products  28 us (8%)
  local copies, waits for them, and re-layouts  24.8 us (7%)
  other arithmetic  18.9 us (5%)
    all_to_all x1, waiting for transfers between devices, body(): u_next = lax.all_to_all(top, MEMBER, 0, 0)  50.2 us
    all_to_all x2, waiting for transfers between devices, summed_rows(): lax.all_to_all(nearer.astype(jnp.bfloat16), far, split_axis=0, concat_axi...  42.3 us
    all_to_all x4, waiting for transfers between devices, sent_and_summed(): lax.all_to_all(tiles, axis, split_axis=0, concat_axis=0, tiled=True)  39.6 us
    all_to_all x2, blocking collectives, sent_to_all(): return lax.all_to_all(copies, axis, split_axis=0, concat_axis=0, tiled=True)  39.4 us
    all_to_all x4, waiting for transfers between devices, sent_to_all(): return lax.all_to_all(copies, axis, split_axis=0, concat_axis=0, tiled=True)  36.7 us
    all_to_all x4, starting transfers between devices, sent_to_all(): return lax.all_to_all(copies, axis, split_axis=0, concat_axis=0, tiled=True)  22.2 us
    all_to_all x4, starting transfers between devices, sent_and_summed(): lax.all_to_all(tiles, axis, split_axis=0, concat_axis=0, tiled=True)  17.9 us
    all_to_all x2, starting transfers between devices, summed_rows(): lax.all_to_all(nearer.astype(jnp.bfloat16), far, split_axis=0, concat_axi...  14.4 us
  transfers between devices with their start and end apart: 11, of which 9 were waited for; matrix products, arithmetic and copies ran while one was open for 9% of the time, Pallas kernels for 0%

profile of v1, /device:TPU:8, one launch (start us, length us, event | category | flops | bytes accessed | tf_op | source)
XLA Modules:
  0.0 353.1 jit_solution(1773057368930031989)
XLA Ops:
  1.8 31.0 %all_to_all.72 = bf16[8,128,1024]{2,1,0:T(8,128)(2,1)S(1)} all-to-all(bf16[8,128,1024]{2,1,0:T(8,128)(2,1)S(1)} %broadcast_in_dim.36), channel_id=1, replica_groups=mesh['member_0'=2,'member_1'=4,'member_2'=2,'dp'=16] {'member_0','member..., dimensions={0} | all-to-all | bytes 4194304 | tf_op jit(solution)/shard_map/all_to_all | solution.py:14
  33.5 8.3 %all_to_all.73 = bf16[2,8,128,1024]{3,2,1,0:T(8,128)(2,1)} all-to-all(bf16[2,8,128,1024]{3,2,1,0:T(8,128)(2,1)S(1)} %broadcast_in_dim.37), channel_id=1, replica_groups=mesh['member_0'=2,'member_1'=4,'member_2'=2,'dp'=16] {'member_2'}, dimensions={0} | all-to-all | bytes 8388608 | tf_op jit(solution)/shard_map/all_to_all | solution.py:14
  44.3 5.9 %all-to-all-start.2 = ((bf16[16,64,2048]{2,1,0:T(8,128)(2,1)}), bf16[16,64,2048]{2,1,0:T(8,128)(2,1)}, u32[]{:S(2)}, u32[]{:S(2)}) async-start(bf16[16,64,2048]{2,1,0:T(8,128)(2,1)} %stack.2), calls=%async_computation.2 | async-start | bytes 8388608 | tf_op jit(solution)/shard_map/all_to_all | solution.py:108
  50.8 4.8 %copy.27 = bf16[2,8,128,1024]{3,2,0,1:T(8,128)(2,1)} copy(bf16[2,8,128,1024]{3,2,1,0:T(8,128)(2,1)} %all_to_all.73) | data formatting | bytes 8388608 | tf_op jit(solution)/shard_map/all_to_all | solution.py:14
  55.6 50.2 %all-to-all-done.2 = bf16[16,64,2048]{2,1,0:T(8,128)(2,1)} async-done(((bf16[16,64,2048]{2,1,0:T(8,128)(2,1)}), bf16[16,64,2048]{2,1,0:T(8,128)(2,1)}, u32[]{:S(2)}, u32[]{:S(2)}) %all-to-all-start.2) | async-done | bytes 4194336 | tf_op jit(solution)/shard_map/all_to_all | solution.py:108
  105.8 4.3 %fusion.37 = f32[394,2048]{1,0:T(8,128)S(1)} fusion(bf16[1024,2048]{1,0:T(8,128)(2,1)} %bitcast.7, bf16[394,1024]{1,0:T(8,128)(2,1)S(1)} %copy-done.1, f32[1024]{0:T(1024)S(1)} %bitcast.61, f32[1024]{0:T(1024)S(1)} %copy-done.6, f32[394]{0:T(512)S(1)} %add_rsqrt_fusion, f32[394]{0:T(512)S(1)} %broadcast_multiply_fusion.2), kind=kOutput, calls=%fused_computation.60 | convolution fusion | flops 1654976512 | bytes 8240208 | tf_op jit(solution)/shard_map/dot_general | solution.py:110
  112.6 4.2 %multiply_reduce_fusion = (f32[2048]{0:T(1024)S(1)}, f32[2048]{0:T(1024)S(1)}, f32[394,2048]{1,0:T(8,128)S(1)}) fusion(f32[394,2048]{1,0:T(8,128)S(1)} %fusion.37, f32[2048]{0:T(1024)S(1)} %bitcast.66, f32[2048]{0:T(1024)S(1)} %bitcast.71, bf16[2048,1024]{1,0:T(8,128)(2,1)S(1)} %bitcast.54, bf16[1,394,1024]{2,1,0:T(8,128)(2,1)S(1)} %copy-done.3, ...), kind=kOutput, calls=%fused_computation.12 | convolution fusion | flops 1673934848 | bytes 11493376 | tf_op jit(solution)/shard_map/dot_general | solution.py:118
  116.8 7.6 %fusion.22 = (f32[1024]{0:T(1024)S(1)}, f32[394]{0:T(512)S(1)}, f32[1024]{0:T(1024)S(1)}, f32[394]{0:T(512)S(1)}, f32[394,1024]{1,0:T(8,128)}) fusion(bf16[394,1024]{1,0:T(8,128)(2,1)S(1)} %copy-done.1, f32[1024]{0:T(1024)S(1)} %bitcast.62, f32[394]{0:T(512)S(1)} %add_rsqrt_fusion, f32[394]{0:T(512)S(1)} %broadcast_multiply_fusion.2, ...), kind=kOutput, calls=%fused_computation.37 | convolution fusion | flops 1675549952 | bytes 13109408 | tf_op jit(solution)/shard_map/dot_general | solution.py:142
  124.4 4.5 %convolution_convert_fusion.1 = bf16[1024,2048]{1,0:T(8,128)(2,1)S(1)} fusion(f32[2048]{0:T(1024)S(1)} %bitcast.68, bf16[394,1024]{1,0:T(8,128)(2,1)S(1)} %copy-done.1, f32[1024]{0:T(1024)S(1)} %bitcast.63, f32[1024]{0:T(1024)S(1)} %copy-done.6, f32[394]{0:T(512)S(1)} %add_rsqrt_fusion, f32[394]{0:T(512)S(1)} %broadcast_multiply_fusion.2, ...), kind=kOutput, calls=%fused_computation.5 | convolution fusion | flops 1674825728 | bytes 11484240 | tf_op jit(solution)/shard_map/dot_general | solution.py:89
  128.9 5.0 %convolution_convert_fusion = bf16[2048,1024]{1,0:T(8,128)(2,1)} fusion(bf16[1,394,1024]{2,1,0:T(8,128)(2,1)S(1)} %copy-done.3, f32[1024]{0:T(1024)S(1)} %bitcast.76, f32[2048]{0:T(1024)S(1)} %bitcast.74, f32[394,2048]{1,0:T(8,128)S(1)} %fusion.37, f32[2048]{0:T(1024)S(1)} %bitcast.69), kind=kOutput, calls=%fused_computation.4 | convolution fusion | flops 1664739328 | bytes 8249344 | tf_op jit(solution)/shard_map/dot_general | solution.py:89
  136.2 5.6 %all-to-all-start.4 = ((bf16[2,8,64,2048]{3,2,1,0:T(8,128)(2,1)}), bf16[2,8,64,2048]{3,2,1,0:T(8,128)(2,1)}, u32[]{:S(2)}, u32[]{:S(2)}) async-start(bf16[2,8,64,2048]{3,2,1,0:T(8,128)(2,1)} %bitcast.51), calls=%async_computation.4 | async-start | bytes 8388608 | tf_op jit(solution)/shard_map/all_to_all | solution.py:36
  141.8 4.8 %copy.44 = bf16[8,2,128,1024]{3,2,0,1:T(8,128)(2,1)} copy(bf16[8,2,128,1024]{3,2,1,0:T(8,128)(2,1)} %bitcast.55) | data formatting | bytes 8388608 | tf_op jit(solution)/shard_map/reshape;reshape | solution.py:31
  146.6 11.9 %all_to_all.74 = bf16[2,8,128,1024]{3,2,1,0:T(8,128)(2,1)} all-to-all(bf16[2,8,128,1024]{3,2,1,0:T(8,128)(2,1)} %bitcast.52), channel_id=1, replica_groups=mesh['member_0'=2,'member_1'=4,'member_2'=2,'dp'=16] {'member_2'}, dimensions={0} | all-to-all | bytes 8388608 | tf_op jit(solution)/shard_map/all_to_all | solution.py:36
  159.5 10.3 %all-to-all-start.12 = ((f32[16,1,7168]{2,1,0:T(1,128)}), f32[16,1,7168]{2,1,0:T(1,128)S(1)}, u32[]{:S(2)}, u32[]{:S(2)}) async-start(f32[16,1,7168]{2,1,0:T(1,128)} %broadcast_in_dim.40), calls=%async_computation.12 | async-start | bytes 917504 | tf_op jit(solution)/shard_map/all_to_all | solution.py:14
  173.3 14.5 %all-to-all-done.12 = f32[16,1,7168]{2,1,0:T(1,128)S(1)} async-done(((f32[16,1,7168]{2,1,0:T(1,128)}), f32[16,1,7168]{2,1,0:T(1,128)S(1)}, u32[]{:S(2)}, u32[]{:S(2)}) %all-to-all-start.12) | async-done | bytes 458784 | tf_op jit(solution)/shard_map/all_to_all | solution.py:14
  187.9 5.2 %all-to-all-start.3 = ((bf16[16,394,64]{1,2,0:T(8,128)(2,1)}), bf16[16,394,64]{1,2,0:T(8,128)(2,1)S(1)}, u32[]{:S(2)}, u32[]{:S(2)}) async-start(bf16[16,394,64]{1,2,0:T(8,128)(2,1)} %bitcast.10), calls=%async_computation.3 | async-start | bytes 2097152 | tf_op jit(solution)/shard_map/all_to_all | solution.py:36
  194.0 14.2 %all-to-all-done.3 = bf16[16,394,64]{1,2,0:T(8,128)(2,1)S(1)} async-done(((bf16[16,394,64]{1,2,0:T(8,128)(2,1)}), bf16[16,394,64]{1,2,0:T(8,128)(2,1)S(1)}, u32[]{:S(2)}, u32[]{:S(2)}) %all-to-all-start.3) | async-done | bytes 806944 | tf_op jit(solution)/shard_map/all_to_all | solution.py:36
  208.9 4.8 %all-to-all-start.13 = ((f32[16,1,1024]{2,1,0:T(1,128)}), f32[16,1,1024]{2,1,0:T(1,128)S(1)}, u32[]{:S(2)}, u32[]{:S(2)}) async-start(f32[16,1,1024]{2,1,0:T(1,128)} %broadcast_in_dim.45), calls=%async_computation.13 | async-start | bytes 131072 | tf_op jit(solution)/shard_map/all_to_all | solution.py:14
  213.7 5.2 %reduce_sum.188 = bf16[8,64,2048]{2,1,0:T(8,128)(2,1)} reduce(bf16[2,8,64,2048]{3,2,1,0:T(8,128)(2,1)} %all-to-all-done.4, bf16[]{:T(256)} %constant.28.clone.1), dimensions={0}, to_apply=%region_5.0 | reduce | flops 1048576 | bytes 6291458 | tf_op jit(solution)/shard_map/reduce_sum | solution.py:37
  218.8 5.7 %all-to-all-start.5 = ((bf16[8,64,2048]{2,1,0:T(8,128)(2,1)}), bf16[8,64,2048]{2,1,0:T(8,128)(2,1)S(1)}, u32[]{:S(2)}, u32[]{:S(2)}) async-start(bf16[8,64,2048]{2,1,0:T(8,128)(2,1)} %reduce_sum.188), calls=%async_computation.5 | async-start | bytes 4194304 | tf_op jit(solution)/shard_map/all_to_all | solution.py:44
  224.6 5.2 %reduce_sum.191 = bf16[8,128,1024]{2,1,0:T(8,128)(2,1)} reduce(bf16[2,8,128,1024]{3,2,1,0:T(8,128)(2,1)} %all_to_all.74, bf16[]{:T(256)} %constant.28.clone.1), dimensions={0}, to_apply=%region_8.0 | reduce | flops 1048576 | bytes 6291458 | tf_op jit(solution)/shard_map/reduce_sum | solution.py:37
  229.8 20.5 %all-to-all-done.5 = bf16[8,64,2048]{2,1,0:T(8,128)(2,1)S(1)} async-done(((bf16[8,64,2048]{2,1,0:T(8,128)(2,1)}), bf16[8,64,2048]{2,1,0:T(8,128)(2,1)S(1)}, u32[]{:S(2)}, u32[]{:S(2)}) %all-to-all-start.5) | async-done | bytes 2097184 | tf_op jit(solution)/shard_map/all_to_all | solution.py:44
  251.6 8.7 %all-to-all-start.9 = ((bf16[8,128,1024]{2,1,0:T(8,128)(2,1)}), bf16[8,128,1024]{2,1,0:T(8,128)(2,1)S(1)}, u32[]{:S(2)}, u32[]{:S(2)}) async-start(bf16[8,128,1024]{2,1,0:T(8,128)(2,1)} %reduce_sum.191), calls=%async_computation.9 | async-start | bytes 4194304 | tf_op jit(solution)/shard_map/all_to_all | solution.py:44
  263.1 21.8 %all-to-all-done.9 = bf16[8,128,1024]{2,1,0:T(8,128)(2,1)S(1)} async-done(((bf16[8,128,1024]{2,1,0:T(8,128)(2,1)}), bf16[8,128,1024]{2,1,0:T(8,128)(2,1)S(1)}, u32[]{:S(2)}, u32[]{:S(2)}) %all-to-all-start.9) | async-done | bytes 2097184 | tf_op jit(solution)/shard_map/all_to_all | solution.py:44
  284.9 3.5 %all-to-all-start.6 = ((bf16[16,4,2048]{2,1,0:T(4,128)(2,1)}), bf16[16,4,2048]{2,1,0:T(4,128)(2,1)S(1)}, u32[]{:S(2)}, u32[]{:S(2)}) async-start(bf16[16,4,2048]{2,1,0:T(4,128)(2,1)} %reshape.76), calls=%async_computation.6 | async-start | bytes 524288 | tf_op jit(solution)/shard_map/all_to_all | solution.py:36
  289.5 13.0 %all-to-all-done.6 = bf16[16,4,2048]{2,1,0:T(4,128)(2,1)S(1)} async-done(((bf16[16,4,2048]{2,1,0:T(4,128)(2,1)}), bf16[16,4,2048]{2,1,0:T(4,128)(2,1)S(1)}, u32[]{:S(2)}, u32[]{:S(2)}) %all-to-all-start.6) | async-done | bytes 262176 | tf_op jit(solution)/shard_map/all_to_all | solution.py:36
  302.5 3.5 %all-to-all-start.10 = ((bf16[16,8,1024]{2,1,0:T(8,128)(2,1)}), bf16[16,8,1024]{2,1,0:T(8,128)(2,1)S(1)}, u32[]{:S(2)}, u32[]{:S(2)}) async-start(bf16[16,8,1024]{2,1,0:T(8,128)(2,1)} %bitcast.15), calls=%async_computation.10 | async-start | bytes 524288 | tf_op jit(solution)/shard_map/all_to_all | solution.py:36
  306.2 12.4 %all-to-all-done.10 = bf16[16,8,1024]{2,1,0:T(8,128)(2,1)S(1)} async-done(((bf16[16,8,1024]{2,1,0:T(8,128)(2,1)}), bf16[16,8,1024]{2,1,0:T(8,128)(2,1)S(1)}, u32[]{:S(2)}, u32[]{:S(2)}) %all-to-all-start.10) | async-done | bytes 262176 | tf_op jit(solution)/shard_map/all_to_all | solution.py:36
  319.4 3.5 %all-to-all-start.7 = ((bf16[16,4,2048]{2,1,0:T(4,128)(2,1)}), bf16[16,4,2048]{2,1,0:T(4,128)(2,1)S(1)}, u32[]{:S(2)}, u32[]{:S(2)}) async-start(bf16[16,4,2048]{2,1,0:T(4,128)(2,1)} %broadcast_in_dim.38), calls=%async_computation.7 | async-start | bytes 524288 | tf_op jit(solution)/shard_map/all_to_all | solution.py:14
  323.0 12.5 %all-to-all-done.7 = bf16[16,4,2048]{2,1,0:T(4,128)(2,1)S(1)} async-done(((bf16[16,4,2048]{2,1,0:T(4,128)(2,1)}), bf16[16,4,2048]{2,1,0:T(4,128)(2,1)S(1)}, u32[]{:S(2)}, u32[]{:S(2)}) %all-to-all-start.7) | async-done | bytes 262176 | tf_op jit(solution)/shard_map/all_to_all | solution.py:14
  336.2 3.5 %all-to-all-start.11 = ((bf16[16,8,1024]{2,1,0:T(8,128)(2,1)}), bf16[16,8,1024]{2,1,0:T(8,128)(2,1)S(1)}, u32[]{:S(2)}, u32[]{:S(2)}) async-start(bf16[16,8,1024]{2,1,0:T(8,128)(2,1)} %broadcast_in_dim.39), calls=%async_computation.11 | async-start | bytes 524288 | tf_op jit(solution)/shard_map/all_to_all | solution.py:14
  342.6 9.7 %all-to-all-done.11 = bf16[16,8,1024]{2,1,0:T(8,128)(2,1)S(1)} async-done(((bf16[16,8,1024]{2,1,0:T(8,128)(2,1)}), bf16[16,8,1024]{2,1,0:T(8,128)(2,1)S(1)}, u32[]{:S(2)}, u32[]{:S(2)}) %all-to-all-start.11) | async-done | bytes 262176 | tf_op jit(solution)/shard_map/all_to_all | solution.py:14
  (55 shorter events, 26.2 us)
Async XLA Ops:
  33.5 8.4 %copy-start.4 = (bf16[64,2048]{1,0:T(8,128)(2,1)S(1)}, bf16[64,2048]{1,0:T(8,128)(2,1)}, u32[]{:S(2)}) copy-start(bf16[64,2048]{1,0:T(8,128)(2,1)} %param.11) | copy-start | bytes 786436
  44.3 5.9 %copy-start.1 = (bf16[394,1024]{1,0:T(8,128)(2,1)S(1)}, bf16[394,1024]{1,0:T(8,128)(2,1)}, u32[]{:S(2)}) copy-start(bf16[394,1024]{1,0:T(8,128)(2,1)} %param.9) | copy-start | bytes 2420740
  44.3 61.4 %all-to-all-start.2 = ((bf16[16,64,2048]{2,1,0:T(8,128)(2,1)}), bf16[16,64,2048]{2,1,0:T(8,128)(2,1)}, u32[]{:S(2)}, u32[]{:S(2)}) async-start(bf16[16,64,2048]{2,1,0:T(8,128)(2,1)} %stack.2), calls=%async_computation.2 | async-start | bytes 8388608 | tf_op jit(solution)/shard_map/all_to_all | solution.py:108
  50.8 55.0 %copy-start.5 = (f32[1,1024]{1,0:T(1,128)S(1)}, f32[1,1024]{1,0:T(1,128)}, u32[]{:S(2)}) copy-start(f32[1,1024]{1,0:T(1,128)} %param.13) | copy-start | bytes 12292
  50.8 55.0 %copy-start.6 = (f32[1024]{0:T(1024)S(1)}, f32[1024]{0:T(1024)}, u32[]{:S(2)}) copy-start(f32[1024]{0:T(1024)} %param.10) | copy-start | bytes 12292
  105.8 4.4 %copy-start.2 = (bf16[2,8,128,1024]{3,2,0,1:T(8,128)(2,1)S(1)}, bf16[2,8,128,1024]{3,2,0,1:T(8,128)(2,1)}, u32[]{:S(2)}) copy-start(bf16[2,8,128,1024]{3,2,0,1:T(8,128)(2,1)} %copy.27) | copy-start | bytes 12582916
  105.8 4.4 %copy-start.3 = (bf16[1,394,1024]{2,1,0:T(8,128)(2,1)S(1)}, bf16[1,394,1024]{2,1,0:T(8,128)(2,1)}, u32[]{:S(2)}) copy-start(bf16[1,394,1024]{2,1,0:T(8,128)(2,1)} %param.17) | copy-start | bytes 2420740
  105.8 4.4 %copy-start.7 = (f32[1,2048]{1,0:T(1,128)S(1)}, f32[1,2048]{1,0:T(1,128)}, u32[]{:S(2)}) copy-start(f32[1,2048]{1,0:T(1,128)} %param.14) | copy-start | bytes 24580
  105.8 4.4 %copy-start.8 = (f32[1,2048]{1,0:T(1,128)S(1)}, f32[1,2048]{1,0:T(1,128)}, u32[]{:S(2)}) copy-start(f32[1,2048]{1,0:T(1,128)} %param.15) | copy-start | bytes 24580
  110.2 2.4 copy-start.9
  136.2 10.4 %all-to-all-start.4 = ((bf16[2,8,64,2048]{3,2,1,0:T(8,128)(2,1)}), bf16[2,8,64,2048]{3,2,1,0:T(8,128)(2,1)}, u32[]{:S(2)}, u32[]{:S(2)}) async-start(bf16[2,8,64,2048]{3,2,1,0:T(8,128)(2,1)} %bitcast.51), calls=%async_computation.4 | async-start | bytes 8388608 | tf_op jit(solution)/shard_map/all_to_all | solution.py:36
  159.5 28.4 %all-to-all-start.12 = ((f32[16,1,7168]{2,1,0:T(1,128)}), f32[16,1,7168]{2,1,0:T(1,128)S(1)}, u32[]{:S(2)}, u32[]{:S(2)}) async-start(f32[16,1,7168]{2,1,0:T(1,128)} %broadcast_in_dim.40), calls=%async_computation.12 | async-start | bytes 917504 | tf_op jit(solution)/shard_map/all_to_all | solution.py:14
  187.9 20.3 %all-to-all-start.3 = ((bf16[16,394,64]{1,2,0:T(8,128)(2,1)}), bf16[16,394,64]{1,2,0:T(8,128)(2,1)S(1)}, u32[]{:S(2)}, u32[]{:S(2)}) async-start(bf16[16,394,64]{1,2,0:T(8,128)(2,1)} %bitcast.10), calls=%async_computation.3 | async-start | bytes 2097152 | tf_op jit(solution)/shard_map/all_to_all | solution.py:36
  208.9 10.0 %all-to-all-start.13 = ((f32[16,1,1024]{2,1,0:T(1,128)}), f32[16,1,1024]{2,1,0:T(1,128)S(1)}, u32[]{:S(2)}, u32[]{:S(2)}) async-start(f32[16,1,1024]{2,1,0:T(1,128)} %broadcast_in_dim.45), calls=%async_computation.13 | async-start | bytes 131072 | tf_op jit(solution)/shard_map/all_to_all | solution.py:14
  218.8 31.5 %all-to-all-start.5 = ((bf16[8,64,2048]{2,1,0:T(8,128)(2,1)}), bf16[8,64,2048]{2,1,0:T(8,128)(2,1)S(1)}, u32[]{:S(2)}, u32[]{:S(2)}) async-start(bf16[8,64,2048]{2,1,0:T(8,128)(2,1)} %reduce_sum.188), calls=%async_computation.5 | async-start | bytes 4194304 | tf_op jit(solution)/shard_map/all_to_all | solution.py:44
  250.3 1.3 copy-start
  251.6 33.2 %all-to-all-start.9 = ((bf16[8,128,1024]{2,1,0:T(8,128)(2,1)}), bf16[8,128,1024]{2,1,0:T(8,128)(2,1)S(1)}, u32[]{:S(2)}, u32[]{:S(2)}) async-start(bf16[8,128,1024]{2,1,0:T(8,128)(2,1)} %reduce_sum.191), calls=%async_computation.9 | async-start | bytes 4194304 | tf_op jit(solution)/shard_map/all_to_all | solution.py:44
  284.9 17.6 %all-to-all-start.6 = ((bf16[16,4,2048]{2,1,0:T(4,128)(2,1)}), bf16[16,4,2048]{2,1,0:T(4,128)(2,1)S(1)}, u32[]{:S(2)}, u32[]{:S(2)}) async-start(bf16[16,4,2048]{2,1,0:T(4,128)(2,1)} %reshape.76), calls=%async_computation.6 | async-start | bytes 524288 | tf_op jit(solution)/shard_map/all_to_all | solution.py:36
  302.5 16.1 %all-to-all-start.10 = ((bf16[16,8,1024]{2,1,0:T(8,128)(2,1)}), bf16[16,8,1024]{2,1,0:T(8,128)(2,1)S(1)}, u32[]{:S(2)}, u32[]{:S(2)}) async-start(bf16[16,8,1024]{2,1,0:T(8,128)(2,1)} %bitcast.15), calls=%async_computation.10 | async-start | bytes 524288 | tf_op jit(solution)/shard_map/all_to_all | solution.py:36
  319.4 16.1 %all-to-all-start.7 = ((bf16[16,4,2048]{2,1,0:T(4,128)(2,1)}), bf16[16,4,2048]{2,1,0:T(4,128)(2,1)S(1)}, u32[]{:S(2)}, u32[]{:S(2)}) async-start(bf16[16,4,2048]{2,1,0:T(4,128)(2,1)} %broadcast_in_dim.38), calls=%async_computation.7 | async-start | bytes 524288 | tf_op jit(solution)/shard_map/all_to_all | solution.py:14
  336.2 16.1 %all-to-all-start.11 = ((bf16[16,8,1024]{2,1,0:T(8,128)(2,1)}), bf16[16,8,1024]{2,1,0:T(8,128)(2,1)S(1)}, u32[]{:S(2)}, u32[]{:S(2)}) async-start(bf16[16,8,1024]{2,1,0:T(8,128)(2,1)} %broadcast_in_dim.39), calls=%async_computation.11 | async-start | bytes 524288 | tf_op jit(solution)/shard_map/all_to_all | solution.py:14
